TPU v7x, 128 devices: a whole 4x4x4 slice. The times are simulated.
128 devices in a mesh: gx: 16 (over x, y), gy: 8 (over z, core).
Axes of the slice: x: 4, y: 4, z: 4, core: 2. Of those that a mesh axis runs over, the one named last changes fastest.
Arguments:
- ocean_heat_field: float32 [16, 384, 128, 128], P('gy', 'gx'), may hold values from -6 to 6
- patch_zone: int32 [384], replicated, may hold values from 0 to 127, as said below
- patch_position: int32 [384], replicated, may hold values from 0 to 5, as said below
- quarter_spins: int32 [384], replicated, may hold values from 0 to 3
- zone_patch_tally: int32 [128], P(('gx', 'gy')), may hold values from 0 to 6, as said below
Outputs:
- regional: float32 [16, 128, 6, 128, 128], P(None, ('gx', 'gy'))
Inputs may be any that keep to these rules, and one draw needn't show every extreme that they name: In each aligned group of 24 blocks no more than 3 go to regions of one column patch_zone // 8, and each group has a column with exactly 3. A region receives at most 6 blocks and some region receives exactly 6. `patch_position`: the blocks of one region have distinct slots 0 to zone_patch_tally of that region minus 1, in increasing block order. zone_patch_tally[r] is the number of blocks j with patch_zone[j] = r.
All inputs are finite; a program needn't handle non-finite values.
Results may differ from a plain program's by a relative error of at most 0.00002.
Values sent between devices are 32-bit elements; how exact they have to be, the bound alone decides.
A program may use at most 128 MiB of HBM per device.

v0:
```python
import jax
import jax.numpy as jnp
from jax import lax
from jax.sharding import PartitionSpec as P


def cut_along(shard, dim, count):
    lengths = shard.shape
    pieces = shard.reshape(*lengths[:dim], count, lengths[dim] // count, *lengths[dim + 1 :])
    return jnp.moveaxis(pieces, dim, 0)


def cut_rows(length, count):
    hop = length // count
    if hop >= 8:
        hop -= hop % 8
    return [hop * k for k in range(1, count)]


def laid_out(pieces, dim):
    lengths = list(pieces.shape[1:])
    lengths[dim] *= pieces.shape[0]
    return jnp.moveaxis(pieces, 0, dim).reshape(lengths)


def cut_exchange(shard, axis, pieces, split_dim, concat_dim):
    blocks = cut_along(shard, split_dim, lax.axis_size(axis))
    split_at = max(range(1, max(2, blocks.ndim - 1)), key=lambda d: blocks.shape[d])
    gathered = []
    for slab in jnp.split(blocks, cut_rows(blocks.shape[split_at], pieces), axis=split_at):
        if slab.size:
            gathered.append(lax.all_to_all(slab, axis, split_axis=0, concat_axis=0, tiled=True))
    return laid_out(jnp.concatenate(gathered, axis=split_at), concat_dim)


def spin_patches(incoming_patches, turn_codes):
    first_turn = jnp.rot90(incoming_patches, 1, axes=(2, 3))
    half_turn = jnp.rot90(incoming_patches, 2, axes=(2, 3))
    last_turn = jnp.rot90(incoming_patches, 3, axes=(2, 3))
    shaped = turn_codes[None, :, None, None]
    return jnp.where(
        shaped == 0,
        incoming_patches,
        jnp.where(shaped == 1, first_turn, jnp.where(shaped == 2, half_turn, last_turn)),
    )


def rank_within(labels, label_count):
    onehot = (labels[:, None] == jnp.arange(label_count, dtype=jnp.int32)[None, :]).astype(
        jnp.int32
    )
    running = jnp.cumsum(onehot, axis=0) - onehot
    return jnp.sum(running * onehot, axis=1)


def on_device(ocean_heat_field, patch_zone, patch_position, quarter_spins, zone_patch_tally):
    epoch_anomalies = ocean_heat_field.shape[0]
    patch_anomalies = ocean_heat_field.shape[1]
    patch_side_length = ocean_heat_field.shape[2]
    column_count = lax.axis_size("gx")
    row_count = lax.axis_size("gy")
    block_total = patch_zone.shape[0]
    per_peer = 2 * patch_anomalies // column_count
    capacity = 2 * patch_anomalies // row_count
    column = patch_zone // row_count
    block_ids = jnp.arange(block_total, dtype=jnp.int32)
    source_group = block_ids // patch_anomalies
    order_rank = rank_within(source_group * column_count + column, column_count * column_count)
    send_place = column * per_peer + order_rank
    my_column = lax.axis_index("gx")
    first_block = my_column * patch_anomalies
    mine_place = lax.dynamic_slice_in_dim(send_place, first_block, patch_anomalies)
    mine_turns = lax.dynamic_slice_in_dim(quarter_spins, first_block, patch_anomalies)
    incoming_patches = ocean_heat_field
    incoming_patches = spin_patches(incoming_patches, mine_turns)
    outgoing = jnp.zeros(
        (epoch_anomalies, column_count * per_peer, patch_side_length, patch_side_length),
        jnp.float32,
    )
    outgoing = outgoing.at[:, mine_place].set(incoming_patches)
    arrived = cut_exchange(outgoing, "gx", 2, 1, 1)
    arrival = source_group * per_peer + order_rank
    row_ids = jnp.arange(row_count, dtype=jnp.int32)[:, None]
    slot_ids = jnp.arange(capacity, dtype=jnp.int32)[None, :]
    targets = ((my_column * row_count + row_ids) * capacity + slot_ids).reshape(-1)
    flat_dest = patch_zone * capacity + patch_position
    matched = flat_dest[None, :] == targets[:, None]
    source = jnp.sum(jnp.where(matched, arrival[None, :] + 1, 0), axis=1) - 1
    present = source >= 0
    picked = jnp.take(arrived, jnp.maximum(source, 0), axis=1)
    picked = jnp.where(present[None, :, None, None], picked, jnp.float32(0.0))
    regional = lax.all_to_all(picked, "gy", split_axis=1, concat_axis=0, tiled=True)
    in_use = jnp.arange(capacity, dtype=jnp.int32) < zone_patch_tally[0]
    regional = jnp.where(in_use[None, :, None, None], regional, jnp.float32(0.0))
    regional = regional - jnp.mean(regional, axis=0, keepdims=True)
    return regional[:, None]


def solution(mesh):
    placed = (P("gy", "gx", None, None), P(), P(), P(), P(("gx", "gy")))
    return jax.shard_map(
        on_device,
        mesh=mesh,
        in_specs=placed,
        out_specs=P(None, ("gx", "gy"), None, None, None),
        check_vma=False,
    )
```

profile of v0, /device:TPU:1, one launch (start us, length us, event | category | flops | bytes accessed | tf_op | source)
XLA Modules:
  0.0 286.4 jit_solution(14438211900863704071)
XLA Ops:
  0.0 2.4 copy.33
  2.4 25.7 %rev.17 = f32[2,24,128,128]{3,2,1,0:T(8,128)} reverse(f32[2,24,128,128]{3,2,1,0:T(8,128)} %param.5), dimensions={2,3} | reverse | bytes 6291456 | tf_op jit(solution)/shard_map/jit(rot90)/jit(_flip)/rev | solution.py:38
  28.1 15.3 %rev.16 = f32[2,24,128,128]{2,3,1,0:T(8,128)} reverse(f32[2,24,128,128]{2,3,1,0:T(8,128)S(1)} %copy.33), dimensions={3} | reverse | bytes 6291456 | tf_op jit(solution)/shard_map/jit(rot90)/jit(_flip)/rev | solution.py:37
  43.4 17.0 %rev.18 = f32[2,24,128,128]{3,2,1,0:T(8,128)} reverse(f32[2,24,128,128]{3,2,1,0:T(8,128)S(1)} %bitcast.43), dimensions={3} | reverse | bytes 6291456 | tf_op jit(solution)/shard_map/jit(rot90)/jit(_flip)/rev | solution.py:39
  60.4 0.8 broadcast_compare_fusion.2
  61.2 6.2 %fusion.2 = f32[24,2,128,128]{3,2,0,1:T(8,128)S(1)} fusion(f32[2,24,128,128]{3,2,1,0:T(8,128)} %param.5, f32[2,24,128,128]{2,3,1,0:T(8,128)} %rev.16, f32[2,24,128,128]{3,2,1,0:T(8,128)} %rev.17, f32[2,24,128,128]{3,2,1,0:T(8,128)} %rev.18, pred[24]{0:T(512)(128)(4,1)S(1)} %get-tuple-element.14, pred[24]{0:T(512)(128)(4,1)S(1)} %get-tuple-element.13, ...), kind=kLoop, calls=%fused_computation.10 | loop fusion | flops 2359296 | bytes 15728712 | tf_op jit(solution)/shard_map/jit(_where)/select_n | solution.py:41
  67.3 0.0 copy-start.1
  67.4 0.0 copy-start.2
  67.4 0.2 copy.35
  67.6 0.4 copy-done.1
  68.0 0.0 copy-done.2
  68.1 0.1 copy.31
  68.2 0.2 fusion.3
  68.4 0.0 copy-start
  68.4 0.8 copy-done
  69.2 1.1 broadcast_add_fusion
  70.4 0.1 copy.32
  70.5 0.2 fusion.6
  70.7 0.1 compare_select_fusion
  70.8 3.5 %broadcast_in_dim.88 = f32[2,48,128,128]{3,2,1,0:T(8,128)} broadcast(f32[]{:T(128)} %constant.69.clone.1), dimensions={} | broadcast | bytes 6291460 | tf_op jit(solution)/shard_map/broadcast_in_dim | solution.py:76
  74.3 6.4 %scatter_fusion = f32[2,48,128,128]{3,2,1,0:T(8,128)} fusion(f32[2,48,128,128]{3,2,1,0:T(8,128)} %broadcast_in_dim.88, s32[24]{0:T(128)S(1)} %compare_select_fusion, f32[24,2,128,128]{3,2,1,0:T(8,128)S(1)} %copy.35), kind=kCustom, calls=%fused_computation.1 | custom fusion | bytes 9437280 | tf_op jit(solution)/shard_map/scatter | solution.py:80
  80.7 3.2 %copy.43 = f32[2,16,3,128,128]{4,3,2,0,1:T(8,128)S(1)} copy(f32[2,16,3,128,128]{4,3,2,1,0:T(8,128)} %bitcast.42) | data formatting | bytes 12582912 | tf_op jit(solution)/shard_map/reshape | solution.py:9
  83.9 2.5 fusion.14
  86.4 45.3 %all_to_all.28 = f32[16,2,3,64,128]{4,3,2,1,0:T(8,128)S(1)} all-to-all(f32[16,2,3,64,128]{4,3,2,1,0:T(8,128)S(1)} %get-tuple-element.7), channel_id=1, replica_groups=mesh['gx'=16,'gy'=8] {'gx'}, dimensions={0} | all-to-all | bytes 6291456 | tf_op jit(solution)/shard_map/all_to_all | solution.py:32
  131.8 4.5 %all-to-all-start.1 = ((f32[16,2,3,64,128]{4,3,2,1,0:T(8,128)}), f32[16,2,3,64,128]{4,3,2,1,0:T(8,128)}, u32[]{:S(2)}, u32[]{:S(2)}) async-start(f32[16,2,3,64,128]{4,3,2,1,0:T(8,128)} %get-tuple-element.8), calls=%async_computation.1 | async-start | bytes 6291456 | tf_op jit(solution)/shard_map/all_to_all | solution.py:32
  136.3 0.1 iota_add_fusion
  136.3 0.1 add.94
  136.4 0.2 select_reduce_fusion.1
  136.6 36.1 %all-to-all-done.1 = f32[16,2,3,64,128]{4,3,2,1,0:T(8,128)} async-done(((f32[16,2,3,64,128]{4,3,2,1,0:T(8,128)}), f32[16,2,3,64,128]{4,3,2,1,0:T(8,128)}, u32[]{:S(2)}, u32[]{:S(2)}) %all-to-all-start.1) | async-done | bytes 3145760 | tf_op jit(solution)/shard_map/all_to_all | solution.py:32
  172.7 2.5 maximum_bitcast_fusion
  175.2 3.1 %copy.37 = f32[2,16,3,128,128]{4,3,2,1,0:T(8,128)} copy(f32[2,16,3,128,128]{4,3,2,0,1:T(8,128)S(1)} %maximum_bitcast_fusion) | data formatting | bytes 12582912 | tf_op jit(solution)/shard_map/transpose | solution.py:23
  178.3 6.4 %gather_fusion = f32[48,2,128,128]{3,2,1,0:T(8,128)} fusion(f32[2,48,128,128]{3,2,1,0:T(8,128)} %bitcast.45, s32[1024]{0:T(1024)S(1)} %pad_clamp_fusion), kind=kCustom, calls=%fused_computation | custom fusion | bytes 12583104 | tf_op jit(solution)/shard_map/jit(_take)/gather | solution.py:90
  184.7 7.0 %select_bitcast_fusion = f32[2,48,128,128]{3,2,0,1:T(8,128)} fusion(f32[48,2,128,128]{3,2,1,0:T(8,128)} %gather_fusion, pred[48]{0:T(512)(128)(4,1)S(1)} %get-tuple-element.16, pred[48]{0:T(512)(128)(4,1)S(1)} %get-tuple-element.15), kind=kLoop, calls=%fused_computation.6 | loop fusion | flops 3145728 | bytes 12583008 | tf_op jit(solution)/shard_map/jit(_where)/select_n | solution.py:91
  191.8 12.2 %all-to-all-start.2 = ((f32[2,48,128,128]{3,2,0,1:T(8,128)}), f32[2,48,128,128]{3,2,0,1:T(8,128)}, u32[]{:S(2)}, u32[]{:S(2)}) async-start(f32[2,48,128,128]{3,2,0,1:T(8,128)} %select_bitcast_fusion), calls=%async_computation.2 | async-start | bytes 12582912 | tf_op jit(solution)/shard_map/all_to_all | solution.py:92
  204.6 70.6 %all-to-all-done.2 = f32[2,48,128,128]{3,2,0,1:T(8,128)} async-done(((f32[2,48,128,128]{3,2,0,1:T(8,128)}), f32[2,48,128,128]{3,2,0,1:T(8,128)}, u32[]{:S(2)}, u32[]{:S(2)}) %all-to-all-start.2) | async-done | bytes 6291488 | tf_op jit(solution)/shard_map/all_to_all | solution.py:92
  275.2 3.2 %copy.38 = f32[2,48,128,128]{3,2,1,0:T(8,128)S(1)} copy(f32[2,48,128,128]{3,2,0,1:T(8,128)} %all-to-all-done.2) | data formatting | bytes 12582912 | tf_op jit(solution)/shard_map/all_to_all | solution.py:92
  278.4 0.7 select_reduce_fusion
  279.2 3.5 %copy.39 = f32[8,2,6,128,128]{4,3,2,1,0:T(8,128)S(1)} copy(f32[8,2,6,128,128]{4,3,1,2,0:T(8,128)} %bitcast.15) | data formatting | bytes 12582912 | tf_op jit(solution)/shard_map/all_to_all | solution.py:92
  282.7 3.7 %fusion = f32[16,1,6,128,128]{4,3,2,0,1:T(8,128)} fusion(f32[8,2,6,128,128]{4,3,2,1,0:T(8,128)S(1)} %copy.39, f32[6,128,128]{2,1,0:T(8,128)S(1)} %broadcast_multiply_fusion, pred[6]{0:T(512)(128)(4,1)S(1)} %iota_compare_fusion.3), kind=kLoop, calls=%fused_computation.4 | loop fusion | flops 3145728 | bytes 12976134 | tf_op jit(solution)/shard_map/sub | solution.py:95
  (11 shorter events, 0.1 us)
Async XLA Ops:
  67.3 0.7 copy-start.1
  67.4 0.7 copy-start.2
  68.4 0.8 copy-start
  131.8 41.0 %all-to-all-start.1 = ((f32[16,2,3,64,128]{4,3,2,1,0:T(8,128)}), f32[16,2,3,64,128]{4,3,2,1,0:T(8,128)}, u32[]{:S(2)}, u32[]{:S(2)}) async-start(f32[16,2,3,64,128]{4,3,2,1,0:T(8,128)} %get-tuple-element.8), calls=%async_computation.1 | async-start | bytes 6291456 | tf_op jit(solution)/shard_map/all_to_all | solution.py:32
  191.8 83.5 %all-to-all-start.2 = ((f32[2,48,128,128]{3,2,0,1:T(8,128)}), f32[2,48,128,128]{3,2,0,1:T(8,128)}, u32[]{:S(2)}, u32[]{:S(2)}) async-start(f32[2,48,128,128]{3,2,0,1:T(8,128)} %select_bitcast_fusion), calls=%async_computation.2 | async-start | bytes 12582912 | tf_op jit(solution)/shard_map/all_to_all | solution.py:92
where the time goes:
time: 289 us; the launch traced here: 286 us
  waiting for transfers between devices  107 us (37%)
  local copies, waits for them, and re-layouts  94.1 us (33%)
  blocking collectives  45.3 us (16%)
  other arithmetic  22.9 us (8%)
  starting transfers between devices  16.7 us (6%)
    all_to_all x1, waiting for transfers between devices, on_device(): lax.all_to_all(picked, 'gy', split_axis=1, concat_axis=0, tiled=True)  70.6 us
    all_to_all x1, blocking collectives, cut_exchange(): lax.all_to_all(slab, axis, split_axis=0, concat_axis=0, tiled=True)  45.3 us
    all_to_all x1, waiting for transfers between devices, cut_exchange(): lax.all_to_all(slab, axis, split_axis=0, concat_axis=0, tiled=True)  36.1 us
    rev x1, local copies, waits for them, and re-layouts, spin_patches(): half_turn = jnp.rot90(incoming_patches, 2, axes=(2, 3))  25.7 us
    rev x1, local copies, waits for them, and re-layouts, spin_patches(): last_turn = jnp.rot90(incoming_patches, 3, axes=(2, 3))  17 us
    rev x1, local copies, waits for them, and re-layouts, spin_patches(): first_turn = jnp.rot90(incoming_patches, 1, axes=(2, 3))  15.3 us
    all_to_all x1, starting transfers between devices, on_device(): lax.all_to_all(picked, 'gy', split_axis=1, concat_axis=0, tiled=True)  12.2 us
    select_n x1, other arithmetic, on_device(): picked = jnp.where(present[None, :, None, None], picked, jnp.float32(0.0))  7.01 us
  transfers between devices with their start and end apart: 2, of which 2 were waited for; matrix products, arithmetic and copies ran while one was open for 0% of the time, Pallas kernels for 0%

commit v1 on v0

v1 whole, which is shorter than its diff:
```python
import functools

import jax
import jax.numpy as jnp
from jax import lax
from jax.experimental import pallas as pl
from jax.experimental.pallas import tpu as pltpu
from jax.sharding import PartitionSpec as P

MOST = 3
AHEAD = 3


def flip_lanes(rows):
    lane = lax.broadcasted_iota(jnp.int32, rows.shape, 1)
    return jnp.take_along_axis(rows, rows.shape[1] - 1 - lane, axis=1, mode="promise_in_bounds")


def flip_rows(rows):
    row = lax.broadcasted_iota(jnp.int32, rows.shape, 0)
    return jnp.take_along_axis(rows, rows.shape[0] - 1 - row, axis=0, mode="promise_in_bounds")


def pack_kernel(region_rows, zone, spins, my_base, field, packed, turned):
    times, blocks, side, _ = field.shape
    strips = side // 8
    base = my_base[0]

    def one(j, _):
        mine = zone[base + j] // region_rows

        def count(i, seen):
            return seen + jnp.where(zone[base + i] // region_rows == mine, 1, 0)

        slot = mine * MOST + lax.fori_loop(0, j, count, 0)
        code = spins[base + j]
        for t in range(times):
            tile = field.at[t, j]

            @pl.when(code % 2 == 1)
            def _():
                turned[t] = tile[...].T

            @pl.when(code % 2 == 0)
            def _():
                turned[t] = tile[...]

            for way in range(4):

                @pl.when(code == way)
                def _():
                    for n in range(strips):
                        m = strips - 1 - n if way in (1, 2) else n
                        rows = turned[t, m * 8 : m * 8 + 8, :]
                        if way in (2, 3):
                            rows = flip_lanes(rows)
                        if way in (1, 2):
                            rows = flip_rows(rows)
                        packed[n, slot, t] = rows

        return 0

    lax.fori_loop(0, blocks, one, 0)


def exchange_kernel(
    columns, rows, pick, tally, packed, result, arrived, staged, outgoing, landed, own_sem, out_sem, xs, xr, zs, zr
):
    strips = packed.shape[0]
    times = packed.shape[2]
    capacity = landed.shape[3]
    epochs = rows * times
    column = lax.axis_index("gx")
    row = lax.axis_index("gy")

    barrier = pltpu.get_barrier_semaphore()

    def greet_column(d, _):
        pl.semaphore_signal(barrier, inc=1, device_id={"gx": lax.rem(column + d, columns)})
        return 0

    def greet_row(d, _):
        pl.semaphore_signal(barrier, inc=1, device_id={"gy": lax.rem(row + d, rows)})
        return 0

    lax.fori_loop(1, columns, greet_column, 0)
    lax.fori_loop(1, rows, greet_row, 0)
    own = pltpu.make_async_copy(
        packed.at[:, pl.ds(column * MOST, MOST)], arrived.at[:, pl.ds(column * MOST, MOST)], own_sem
    )
    own.start()
    pl.semaphore_wait(barrier, columns + rows - 2)

    def send_column(n):
        def body(d, _):
            peer = lax.rem(column + d, columns)
            pltpu.make_async_remote_copy(
                src_ref=packed.at[n, pl.ds(peer * MOST, MOST)],
                dst_ref=arrived.at[n, pl.ds(column * MOST, MOST)],
                send_sem=xs.at[n],
                recv_sem=xr.at[n],
                device_id={"gx": peer},
            ).start()
            return 0

        lax.fori_loop(1, columns, body, 0)

    def column_whole(n):
        width = (columns - 1) * MOST
        return pltpu.make_async_remote_copy(
            src_ref=packed.at[n, pl.ds(0, width)],
            dst_ref=arrived.at[n, pl.ds(0, width)],
            send_sem=xs.at[n],
            recv_sem=xr.at[n],
            device_id={"gx": lax.rem(column + 1, columns)},
        )

    def send_row(n):
        def body(d, _):
            peer = lax.rem(row + d, rows)
            pltpu.make_async_remote_copy(
                src_ref=outgoing.at[n, peer],
                dst_ref=landed.at[n, row],
                send_sem=zs.at[n],
                recv_sem=zr.at[n],
                device_id={"gy": peer},
            ).start()
            return 0

        lax.fori_loop(1, rows, body, 0)

    def row_whole(n):
        return pltpu.make_async_remote_copy(
            src_ref=outgoing.at[n, pl.ds(0, rows - 1)],
            dst_ref=landed.at[n, pl.ds(0, rows - 1)],
            send_sem=zs.at[n],
            recv_sem=zr.at[n],
            device_id={"gy": lax.rem(row + 1, rows)},
        )

    def out_copy(n):
        return pltpu.make_async_copy(
            landed.at[n], result.at[:, :, :, pl.ds(n * 8, 8), :], out_sem.at[n]
        )

    def select(n):
        for a in range(columns * MOST):
            for t in range(times):
                staged[a, t] = arrived[n, a, t]
        for r in range(rows):
            for s in range(capacity):
                source = pick[r * capacity + s]
                for t in range(times):
                    outgoing[n, r, t, s] = staged[source, t]
        for t in range(times):
            for s in range(capacity):
                landed[n, row, t, s] = staged[pick[row * capacity + s], t]

    def centre(n):
        row_whole(n).wait_recv()
        for s in range(capacity):
            total = landed[n, 0, 0, s]
            for e in range(1, epochs):
                total = total + landed[n, e // times, e % times, s]
            mean = total * jnp.float32(1.0 / epochs)
            used = s < tally[0]
            for e in range(epochs):
                value = landed[n, e // times, e % times, s]
                landed[n, e // times, e % times, s] = jnp.where(used, value - mean, 0.0)
        out_copy(n).start()

    def ahead(n, _):
        send_column(n)
        return 0

    lax.fori_loop(0, AHEAD, ahead, 0)
    own.wait()

    def step(n, _):
        column_whole(n).wait_recv()
        select(n)

        @pl.when(n + AHEAD < strips)
        def _():
            send_column(n + AHEAD)

        send_row(n)

        @pl.when(n >= 2)
        def _():
            centre(n - 2)

        return 0

    lax.fori_loop(0, strips, step, 0)
    centre(strips - 2)
    centre(strips - 1)

    def drain(n, _):
        column_whole(n).wait_send()
        row_whole(n).wait_send()
        out_copy(n).wait()
        return 0

    lax.fori_loop(0, strips, drain, 0)


def tables(patch_zone, patch_position, columns, rows, capacity):
    zone = patch_zone.reshape(columns, -1)
    column = zone // rows
    blocks = zone.shape[1]
    earlier = jnp.arange(blocks)[None, :, None] > jnp.arange(blocks)[None, None, :]
    same = column[:, :, None] == column[:, None, :]
    rank = jnp.sum(jnp.where(same & earlier, 1, 0), axis=2)
    arrival = (jnp.arange(columns)[:, None] * MOST + rank).reshape(-1)
    target = jnp.arange(rows * capacity) + lax.axis_index("gx") * (rows * capacity)
    place = patch_zone * capacity + patch_position
    return jnp.sum(jnp.where(place[None, :] == target[:, None], arrival[None, :], 0), axis=1).astype(jnp.int32)


def on_device(field, patch_zone, patch_position, spins, tally):
    times, blocks, side, _ = field.shape
    columns = lax.axis_size("gx")
    rows = lax.axis_size("gy")
    capacity = 2 * blocks // rows
    strips = side // 8
    pick = tables(patch_zone, patch_position, columns, rows, capacity)
    base = (lax.axis_index("gx") * blocks).reshape(1).astype(jnp.int32)
    smem = pl.BlockSpec(memory_space=pltpu.SMEM)
    packed = pl.pallas_call(
        functools.partial(pack_kernel, rows),
        out_shape=jax.ShapeDtypeStruct((strips, columns * MOST, times, 8, side), jnp.float32),
        in_specs=[smem, smem, smem, pl.BlockSpec(memory_space=pltpu.VMEM)],
        out_specs=pl.BlockSpec(memory_space=pltpu.VMEM),
        scratch_shapes=[pltpu.VMEM((times, side, side), jnp.float32)],
        name="pack",
    )(patch_zone, spins, base, field)
    result = pl.pallas_call(
        functools.partial(exchange_kernel, columns, rows),
        out_shape=jax.ShapeDtypeStruct((rows, times, capacity, side, side), jnp.float32),
        in_specs=[smem, smem, pl.BlockSpec(memory_space=pl.ANY)],
        out_specs=pl.BlockSpec(memory_space=pl.ANY),
        scratch_shapes=[
            pltpu.VMEM((strips, columns * MOST, times, 8, side), jnp.float32),
            pltpu.VMEM((columns * MOST, times, 8, side), jnp.float32),
            pltpu.VMEM((strips, rows, times, capacity, 8, side), jnp.float32),
            pltpu.VMEM((strips, rows, times, capacity, 8, side), jnp.float32),
            pltpu.SemaphoreType.DMA,
            pltpu.SemaphoreType.DMA((strips,)),
            pltpu.SemaphoreType.DMA((strips,)),
            pltpu.SemaphoreType.DMA((strips,)),
            pltpu.SemaphoreType.DMA((strips,)),
            pltpu.SemaphoreType.DMA((strips,)),
        ],
        compiler_params=pltpu.CompilerParams(collective_id=0, has_side_effects=True),
        name="exchange",
    )(pick, tally, packed)
    return result.reshape(rows * times, 1, capacity, side, side)


def solution(mesh):
    placed = (P("gy", "gx", None, None), P(), P(), P(), P(("gx", "gy")))
    return jax.shard_map(
        on_device,
        mesh=mesh,
        in_specs=placed,
        out_specs=P(None, ("gx", "gy"), None, None, None),
        check_vma=False,
    )
```

time: 289 us -> 115 us (0.40)
  waiting for transfers between devices: 107 us -> 0 us
  Pallas kernels: 0 us -> 104 us
  local copies, waits for them, and re-layouts: 94.1 us -> 7.14 us
  blocking collectives: 45.3 us -> 0 us
  other arithmetic: 22.9 us -> 1.95 us
  starting transfers between devices: 16.7 us -> 0 us
    all_to_all x2 -> x0, waiting for transfers between devices: 107 us -> none  [the longest x1 70.6 us: on_device(): lax.all_to_all(picked, 'gy', split_axis=1, concat_axis=0, tiled=True)]
    pallas_call x0 -> x2, Pallas kernels: none -> 104 us  [the longest x1 91.4 us: on_device(): pl.pallas_call(functools.partial(exchange_kernel, columns, rows), out_sha...]
    rev x3 -> x0, local copies, waits for them, and re-layouts: 58 us -> none  [the longest x1 25.7 us: spin_patches(): half_turn = jnp.rot90(incoming_patches, 2, axes=(2, 3))]
    all_to_all x1 -> x0, blocking collectives: 45.3 us -> none  [cut_exchange(): lax.all_to_all(slab, axis, split_axis=0, concat_axis=0, tiled=True)]
    all_to_all x2 -> x0, starting transfers between devices: 16.7 us -> none  [the longest x1 12.2 us: on_device(): lax.all_to_all(picked, 'gy', split_axis=1, concat_axis=0, tiled=True)]
    select_n x3 -> x1, other arithmetic: 13.3 us -> 0.01 us  [tables(): column = zone // rows]
    all_to_all x2 -> x0, local copies, waits for them, and re-layouts: 6.75 us -> none  [on_device(): lax.all_to_all(picked, 'gy', split_axis=1, concat_axis=0, tiled=True)]
    scatter x1 -> x0, local copies, waits for them, and re-layouts: 6.45 us -> none  [on_device(): outgoing = outgoing.at[:, mine_place].set(incoming_patches)]
  transfers between devices with their start and end apart: 2 -> 0, of which waited for: 2 -> 0; matrix products, arithmetic and copies ran while one was open for 0% -> 0% of each run, Pallas kernels for 0% -> 0%
where the time goes in v1:
time: 115 us; the launch traced here: 114 us
  Pallas kernels  104 us (90%)
  local copies, waits for them, and re-layouts  7.14 us (6%)
  other arithmetic  1.95 us (2%)
    pallas_call x1, Pallas kernels, on_device(): pl.pallas_call(functools.partial(exchange_kernel, columns, rows), out_sha...  91.4 us
    pallas_call x1, Pallas kernels, on_device(): pl.pallas_call(functools.partial(pack_kernel, rows), out_shape=jax.ShapeD...  12.7 us
    unnamed x1, local copies, waits for them, and re-layouts  6.29 us

profile of v1, /device:TPU:1, one launch (start us, length us, event | category | flops | bytes accessed | tf_op | source)
XLA Modules:
  0.0 113.9 jit_solution(5889275211368117635)
XLA Ops:
  0.7 0.7 multiply_add_fusion
  1.4 0.8 reshape.102
  2.2 0.4 select_reduce_fusion
  2.6 0.1 broadcast_add_fusion
  2.7 0.1 add.42
  2.8 0.7 select_reduce_fusion.1.pick
  3.5 12.7 %pack.1.packed = f32[16,48,2,8,128]{4,3,2,1,0:T(8,128)} custom-call(s32[384]{0:T(512)} %zone.1, s32[384]{0:T(512)} %spins.1, s32[1]{0:T(128)} %bitcast.my_base, f32[2,24,128,128]{3,2,1,0:T(8,128)} %field.1), custom_call_target="tpu_custom_call" | custom-call | tf_op jit(solution)/shard_map/pack/pallas_call | solution.py:230
  16.2 91.4 %exchange.1 = f32[8,2,6,128,128]{4,3,2,1,0:T(8,128)} custom-call(s32[48]{0:T(128)} %select_reduce_fusion.1.pick, s32[1]{0:T(128)S(6)} %copy.9.tally, f32[16,48,2,8,128]{4,3,2,1,0:T(8,128)} %pack.1.packed), custom_call_target="tpu_custom_call" | custom-call | tf_op jit(solution)/shard_map/exchange/pallas_call | solution.py:238
  107.6 6.3 %copy.10 = f32[16,1,6,128,128]{4,3,2,1,0:T(8,128)} copy(f32[16,1,6,128,128]{4,3,2,1,0:T(8,128)} %bitcast.4) | data formatting | bytes 12582912
  (4 shorter events, 0.0 us)

commit v2 on v0

v2 whole, which is shorter than its diff:
```python
import functools

import jax
import jax.numpy as jnp
from jax import lax
from jax.experimental import pallas as pl
from jax.experimental.pallas import tpu as pltpu
from jax.sharding import PartitionSpec as P

MOST = 3
AHEAD = 6
TURNS = 3


def gather_lanes(rows, index):
    return jnp.take_along_axis(rows, index, axis=1, mode="promise_in_bounds")


def gather_rows(rows, index):
    return jnp.take_along_axis(rows, index, axis=0, mode="promise_in_bounds")


def maybe_reversed(axis, flip):
    index = lax.broadcasted_iota(jnp.int32, (8, 128), axis)
    return jnp.where(flip, (8, 128)[axis] - 1 - index, index)


def turn(tile, code):
    strips = tile.shape[0] // 8
    cut = [tile[8 * n : 8 * n + 8] for n in range(strips)]
    odd = code % 2 == 1
    half = code == 2
    last = code == 3
    rows_back = jnp.logical_or(code == 1, half)
    lanes = maybe_reversed(1, half)
    flat = [gather_lanes(rows, lanes) for rows in cut]
    before = maybe_reversed(0, last)
    ahead = [gather_rows(jnp.where(last, cut[strips - 1 - n], cut[n]), before) for n in range(strips)]
    crossed = jnp.concatenate(ahead, axis=0).T
    taken = [jnp.where(odd, crossed[8 * n : 8 * n + 8], flat[n]) for n in range(strips)]
    after = maybe_reversed(0, rows_back)
    return [gather_rows(jnp.where(rows_back, taken[strips - 1 - n], taken[n]), after) for n in range(strips)]


def exchange_kernel(
    columns, rows, send, pick, spins, field, result,
    turned, packed, arrived, staged, outgoing, xs, xr, zs, zr,
):
    times, blocks, side, _ = field.shape
    strips = side // 8
    chunks = times * strips
    capacity = outgoing.shape[2]
    column = lax.axis_index("gx")
    row = lax.axis_index("gy")

    barrier = pltpu.get_barrier_semaphore()

    def greet_column(d, _):
        pl.semaphore_signal(barrier, inc=1, device_id={"gx": lax.rem(column + d, columns)})
        return 0

    def greet_row(d, _):
        pl.semaphore_signal(barrier, inc=1, device_id={"gy": lax.rem(row + d, rows)})
        return 0

    lax.fori_loop(1, columns, greet_column, 0)
    lax.fori_loop(1, rows, greet_row, 0)

    def turn_block(t, j):
        strips_of = turn(field[t, j], spins[column * blocks + j])
        for n in range(strips):
            turned[t, n, j] = strips_of[n]

    def turn_first(j, _):
        turn_block(0, 2 * j)
        turn_block(0, 2 * j + 1)
        return 0

    lax.fori_loop(0, blocks // 2, turn_first, 0)

    def pack(m):
        for p in range(columns * MOST):
            packed[m, p] = turned[m // strips, m % strips, send[p]]

    def send_column(m):
        def body(d, _):
            peer = lax.rem(column + d, columns)
            pltpu.make_async_remote_copy(
                src_ref=packed.at[m, pl.ds(peer * MOST, MOST)],
                dst_ref=arrived.at[m, pl.ds(column * MOST, MOST)],
                send_sem=xs.at[m],
                recv_sem=xr.at[m],
                device_id={"gx": peer},
            ).start()
            return 0

        lax.fori_loop(1, columns, body, 0)

    def column_whole(m):
        width = (columns - 1) * MOST
        return pltpu.make_async_remote_copy(
            src_ref=packed.at[m, pl.ds(0, width)],
            dst_ref=arrived.at[m, pl.ds(0, width)],
            send_sem=xs.at[m],
            recv_sem=xr.at[m],
            device_id={"gx": lax.rem(column + 1, columns)},
        )

    def landing(r, m):
        return result.at[r, m // strips, :, pl.ds((m % strips) * 8, 8), :]

    def send_row(m):
        def body(d, _):
            peer = lax.rem(row + d, rows)
            pltpu.make_async_remote_copy(
                src_ref=outgoing.at[m, peer],
                dst_ref=landing(row, m),
                send_sem=zs.at[m],
                recv_sem=zr.at[m],
                device_id={"gy": peer},
            ).start()
            return 0

        lax.fori_loop(1, rows, body, 0)

    def row_whole(m):
        return pltpu.make_async_remote_copy(
            src_ref=outgoing.at[m, pl.ds(0, rows - 1)],
            dst_ref=outgoing.at[m, pl.ds(0, rows - 1)],
            send_sem=zs.at[m],
            recv_sem=zr.at[m],
            device_id={"gy": lax.rem(row + 1, rows)},
        )

    def select(m):
        for a in range(columns * MOST):
            staged[a] = arrived[m, a]
        for q in range(MOST):
            staged[column * MOST + q] = packed[m, column * MOST + q]
        for r in range(rows):
            for s in range(capacity):
                outgoing[m, r, s] = staged[pick[r * capacity + s]]
        here = landing(row, m)
        for s in range(capacity):
            here[s] = outgoing[m, row, s]

    pl.semaphore_wait(barrier, columns + rows - 2)

    def ahead(m, _):
        pack(m)
        send_column(m)
        return 0

    lax.fori_loop(0, AHEAD, ahead, 0)

    def step(m, _):
        @pl.when(m < (times - 1) * blocks // TURNS)
        def _():
            for i in range(TURNS):
                at = m * TURNS + i
                turn_block(1 + at // blocks, at % blocks)

        @pl.when(m + AHEAD < chunks)
        def _():
            pack(m + AHEAD)

        column_whole(m).wait_recv()
        select(m)

        @pl.when(m + AHEAD < chunks)
        def _():
            send_column(m + AHEAD)

        send_row(m)
        return 0

    lax.fori_loop(0, chunks, step, 0)

    def drain(m, _):
        column_whole(m).wait_send()
        row_whole(m).wait()
        return 0

    lax.fori_loop(0, chunks, drain, 0)


def centre_kernel(tally, regional, result, centred, out_sem):
    epochs, capacity, side, _ = regional.shape

    def put(s):
        return pltpu.make_async_copy(centred.at[:, s], result.at[:, s], out_sem.at[s])

    for s in range(capacity):

        @pl.when(s < tally[0])
        def _():
            def strip(n, _):
                at = pl.ds(n * 8, 8)
                values = [regional[e, s, at, :] for e in range(epochs)]
                level = values
                while len(level) > 1:
                    level = [a + b for a, b in zip(level[::2], level[1::2])]
                mean = level[0] * jnp.float32(1.0 / epochs)
                for e in range(epochs):
                    centred[e, s, at, :] = values[e] - mean
                return 0

            lax.fori_loop(0, side // 8, strip, 0, unroll=2)

        @pl.when(s >= tally[0])
        def _():
            def strip(n, _):
                for e in range(epochs):
                    centred[e, s, pl.ds(n * 8, 8), :] = jnp.zeros((8, side), jnp.float32)
                return 0

            lax.fori_loop(0, side // 8, strip, 0, unroll=2)

        put(s).start()
    for s in range(capacity):
        put(s).wait()


def tables(patch_zone, patch_position, columns, rows, capacity):
    total = patch_zone.shape[0]
    blocks = total // columns
    me = lax.axis_index("gx")
    block = jnp.arange(total, dtype=jnp.int32)
    group = block // blocks
    key = group * columns + patch_zone // rows
    before = (key[None, :] == key[:, None]) & (block[None, :] < block[:, None])
    rank = jnp.sum(jnp.where(before, 1, 0), axis=1)
    place = patch_zone * capacity + patch_position - me * (rows * capacity)
    target = jnp.arange(rows * capacity, dtype=jnp.int32)
    pick = jnp.sum(jnp.where(place[None, :] == target[:, None], (group * MOST + rank)[None, :], 0), axis=1)
    slot = jnp.where(group == me, (patch_zone // rows) * MOST + rank, -1)
    out_slot = jnp.arange(columns * MOST, dtype=jnp.int32)
    send = jnp.sum(jnp.where(slot[None, :] == out_slot[:, None], (block - me * blocks)[None, :], 0), axis=1)
    return send.astype(jnp.int32), pick.astype(jnp.int32)


def on_device(field, patch_zone, patch_position, spins, tally):
    times, blocks, side, _ = field.shape
    columns = lax.axis_size("gx")
    rows = lax.axis_size("gy")
    capacity = 2 * blocks // rows
    strips = side // 8
    chunks = times * strips
    send, pick = tables(patch_zone, patch_position, columns, rows, capacity)
    smem = pl.BlockSpec(memory_space=pltpu.SMEM)
    vmem = pl.BlockSpec(memory_space=pltpu.VMEM)
    anywhere = pl.BlockSpec(memory_space=pl.ANY)
    arrived = pl.pallas_call(
        functools.partial(exchange_kernel, columns, rows),
        out_shape=pltpu.VMEM((rows, times, capacity, side, side), jnp.float32),
        in_specs=[smem, smem, smem, vmem],
        out_specs=vmem,
        scratch_shapes=[
            pltpu.VMEM((times, strips, blocks, 8, side), jnp.float32),
            pltpu.VMEM((chunks, columns * MOST, 8, side), jnp.float32),
            pltpu.VMEM((chunks, columns * MOST, 8, side), jnp.float32),
            pltpu.VMEM((columns * MOST, 8, side), jnp.float32),
            pltpu.VMEM((chunks, rows, capacity, 8, side), jnp.float32),
            pltpu.SemaphoreType.DMA((chunks,)),
            pltpu.SemaphoreType.DMA((chunks,)),
            pltpu.SemaphoreType.DMA((chunks,)),
            pltpu.SemaphoreType.DMA((chunks,)),
        ],
        compiler_params=pltpu.CompilerParams(
            collective_id=0, has_side_effects=True, vmem_limit_bytes=36 * 2**20
        ),
        name="exchange",
    )(send, pick, spins, pltpu.with_memory_space_constraint(field, pltpu.VMEM))
    regional = arrived.reshape(rows * times, capacity, side, side)
    centred = pl.pallas_call(
        centre_kernel,
        out_shape=jax.ShapeDtypeStruct((rows * times, capacity, side, side), jnp.float32),
        in_specs=[smem, vmem],
        out_specs=anywhere,
        scratch_shapes=[
            pltpu.VMEM((rows * times, capacity, side, side), jnp.float32),
            pltpu.SemaphoreType.DMA((capacity,)),
        ],
        compiler_params=pltpu.CompilerParams(vmem_limit_bytes=20 * 2**20),
        name="centre",
    )(tally, regional)
    return centred[:, None]


def solution(mesh):
    placed = (P("gy", "gx", None, None), P(), P(), P(), P(("gx", "gy")))
    return jax.shard_map(
        on_device,
        mesh=mesh,
        in_specs=placed,
        out_specs=P(None, ("gx", "gy"), None, None, None),
        check_vma=False,
    )
```

time: 289 us -> 94.4 us (0.33)
  waiting for transfers between devices: 107 us -> 0 us
  local copies, waits for them, and re-layouts: 94.1 us -> 2.57 us
  Pallas kernels: 0 us -> 89.2 us
  blocking collectives: 45.3 us -> 0 us
  other arithmetic: 22.9 us -> 1.77 us
  starting transfers between devices: 16.7 us -> 0 us
    all_to_all x2 -> x0, waiting for transfers between devices: 107 us -> none  [the longest x1 70.6 us: on_device(): lax.all_to_all(picked, 'gy', split_axis=1, concat_axis=0, tiled=True)]
    pallas_call x0 -> x2, Pallas kernels: none -> 89.2 us  [the longest x1 86.3 us: on_device(): pl.pallas_call(functools.partial(exchange_kernel, columns, rows), out_sha...]
    rev x3 -> x0, local copies, waits for them, and re-layouts: 58 us -> none  [the longest x1 25.7 us: spin_patches(): half_turn = jnp.rot90(incoming_patches, 2, axes=(2, 3))]
    all_to_all x1 -> x0, blocking collectives: 45.3 us -> none  [cut_exchange(): lax.all_to_all(slab, axis, split_axis=0, concat_axis=0, tiled=True)]
    all_to_all x2 -> x0, starting transfers between devices: 16.7 us -> none  [the longest x1 12.2 us: on_device(): lax.all_to_all(picked, 'gy', split_axis=1, concat_axis=0, tiled=True)]
    select_n x3 -> x0, other arithmetic: 13.3 us -> none  [the longest x1 7.01 us: on_device(): picked = jnp.where(present[None, :, None, None], picked, jnp.float32(0.0))]
    all_to_all x2 -> x0, local copies, waits for them, and re-layouts: 6.75 us -> none  [on_device(): lax.all_to_all(picked, 'gy', split_axis=1, concat_axis=0, tiled=True)]
    scatter x1 -> x0, local copies, waits for them, and re-layouts: 6.45 us -> none  [on_device(): outgoing = outgoing.at[:, mine_place].set(incoming_patches)]
  transfers between devices with their start and end apart: 2 -> 0, of which waited for: 2 -> 0; matrix products, arithmetic and copies ran while one was open for 0% -> 0% of each run, Pallas kernels for 0% -> 0%
where the time goes in v2:
time: 94.4 us; the launch traced here: 94.2 us
  Pallas kernels  89.2 us (94%)
  local copies, waits for them, and re-layouts  2.57 us (3%)
  other arithmetic  1.77 us (2%)
    pallas_call x1, Pallas kernels, on_device(): pl.pallas_call(functools.partial(exchange_kernel, columns, rows), out_sha...  86.3 us
    pallas_call x1, Pallas kernels, on_device(): pl.pallas_call(centre_kernel, out_shape=jax.ShapeDtypeStruct((rows * time...  2.94 us
    unnamed x4, local copies, waits for them, and re-layouts  2.57 us

profile of v2, /device:TPU:1, one launch (start us, length us, event | category | flops | bytes accessed | tf_op | source)
XLA Modules:
  0.0 94.2 jit_solution(15433350497446943889)
XLA Ops:
  0.7 0.7 add_subtract_fusion
  1.4 0.2 select_reduce_fusion
  1.6 0.7 multiply_add_fusion
  2.3 0.1 select_reduce_fusion.1
  2.4 0.0 copy-start
  2.4 1.9 %copy-done = f32[2,24,128,128]{3,2,1,0:T(8,128)S(1)} copy-done((f32[2,24,128,128]{3,2,1,0:T(8,128)S(1)}, f32[2,24,128,128]{3,2,1,0:T(8,128)}, u32[]{:S(2)}) %copy-start) | copy-done | bytes 3145752
  4.3 0.0 copy-start.1
  4.3 0.7 copy-done.1
  5.0 86.3 %exchange.1 = f32[8,2,6,128,128]{4,3,2,1,0:T(8,128)S(1)} custom-call(s32[48]{0:T(128)S(1)} %get-tuple-element.10.send, s32[48]{0:T(128)S(1)} %get-tuple-element.9.pick, s32[384]{0:T(512)S(1)} %copy-done.1, f32[2,24,128,128]{3,2,1,0:T(8,128)S(1)} %copy-done), custom_call_target="tpu_custom_call" | custom-call | tf_op jit(solution)/shard_map/exchange/pallas_call | solution.py:253
  91.3 2.9 %centre.1 = f32[16,6,128,128]{3,2,1,0:T(8,128)} custom-call(s32[1]{0:T(128)S(6)} %copy.8.tally, f32[16,6,128,128]{3,2,1,0:T(8,128)S(1)} %bitcast.4), custom_call_target="tpu_custom_call" | custom-call | tf_op jit(solution)/shard_map/centre/pallas_call | solution.py:275
  (1 shorter events, 0.0 us)
Async XLA Ops:
  2.4 1.9 %copy-start = (f32[2,24,128,128]{3,2,1,0:T(8,128)S(1)}, f32[2,24,128,128]{3,2,1,0:T(8,128)}, u32[]{:S(2)}) copy-start(f32[2,24,128,128]{3,2,1,0:T(8,128)} %field.1) | copy-start | bytes 9437188
  4.3 0.7 copy-start.1

commit v3 on v2

--- a/solution.py
+++ b/solution.py
@@ -1,4 +1,5 @@
 import functools
+import math
 
 import jax
 import jax.numpy as jnp
@@ -9,7 +10,16 @@
 
 MOST = 3
 AHEAD = 6
+HALF = 64
+PIECES = 4
 TURNS = 3
+
+
+def offsets(columns):
+    width = math.isqrt(columns)
+    far = [min(d, width - d) for d in range(width)]
+    steps = [(dx, dy) for dx in range(width) for dy in range(width) if dx or dy]
+    return sorted(steps, key=lambda step: -(far[step[0]] + far[step[1]]))
 
 
 def gather_lanes(rows, index):
@@ -42,16 +52,65 @@
     return [gather_rows(jnp.where(rows_back, taken[strips - 1 - n], taken[n]), after) for n in range(strips)]
 
 
+def earlier(flat, d):
+    above = jnp.concatenate([flat[:1], flat[:-1]], axis=0)
+    lane = lax.broadcasted_iota(jnp.int32, flat.shape, 1)
+    return jnp.where(lane >= d, pltpu.roll(flat, d, 1), pltpu.roll(above, d, 1))
+
+
+def tables(zone, place, columns, rows, blocks, capacity):
+    me = lax.axis_index("gx")
+    line = lax.broadcasted_iota(jnp.int32, zone.shape, 0) * 128 + lax.broadcasted_iota(jnp.int32, zone.shape, 1)
+    group = line // blocks
+    within = line - group * blocks
+    column = zone // rows
+    rank = jnp.zeros_like(zone)
+    for d in range(1, blocks):
+        rank += jnp.where((within >= d) & (earlier(column, d) == column), 1, 0)
+    place = zone * capacity + place - me * (rows * capacity)
+    place = jnp.where((place >= 0) & (place < rows * capacity), place, -1)
+    slot = jnp.where(group == me, column * MOST + rank + HALF, -1)
+    pad = jnp.full((4 - zone.shape[0], 128), -1, jnp.int32)
+    both = jnp.concatenate([place, pad, slot, pad], axis=0).T
+    values = jnp.concatenate([group * MOST + rank, pad, within, pad], axis=0).T
+    lane = lax.broadcasted_iota(jnp.int32, (128, 128), 1)
+    total = jnp.zeros((128, 128), jnp.int32)
+    for i in range(zone.shape[0]):
+        for k in (i, 4 + i):
+            total += jnp.where(both[:, k : k + 1] == lane, values[:, k : k + 1], 0)
+    found = jnp.sum(total, axis=0, keepdims=True)
+    last = jnp.where(lane[:1] < HALF, columns * MOST - 1, blocks - 1)
+    return jnp.minimum(found, last)
+
+
 def exchange_kernel(
-    columns, rows, send, pick, spins, field, result,
-    turned, packed, arrived, staged, outgoing, xs, xr, zs, zr,
+    columns, rows, zone, place, spins, field, result,
+    zone_v, place_v, table_v, table, turns, loaded, turned, packed, arrived, staged, outgoing,
+    small_sem, load_sem, xs, xr, zs, zr,
 ):
-    times, blocks, side, _ = field.shape
+    times, blocks, side, _ = loaded.shape
     strips = side // 8
     chunks = times * strips
     capacity = outgoing.shape[2]
     column = lax.axis_index("gx")
     row = lax.axis_index("gy")
+    third = blocks // PIECES
+
+    small = [
+        pltpu.make_async_copy(zone, zone_v, small_sem.at[0]),
+        pltpu.make_async_copy(place, place_v, small_sem.at[1]),
+        pltpu.make_async_copy(spins, turns, small_sem.at[2]),
+    ]
+    for copy in small:
+        copy.start()
+
+    def load(t, i):
+        cut = pl.ds(i * third, third)
+        return pltpu.make_async_copy(field.at[t, cut], loaded.at[t, cut], load_sem.at[t, i])
+
+    for t in range(times):
+        for i in range(PIECES):
+            load(t, i).start()
 
     barrier = pltpu.get_barrier_semaphore()
 
@@ -66,25 +125,40 @@
     lax.fori_loop(1, columns, greet_column, 0)
     lax.fori_loop(1, rows, greet_row, 0)
 
+    for copy in small:
+        copy.wait()
+    table_v[...] = tables(zone_v[...], place_v[...], columns, rows, blocks, capacity)
+    to_scalars = pltpu.make_async_copy(table_v, table, small_sem.at[3])
+
     def turn_block(t, j):
-        strips_of = turn(field[t, j], spins[column * blocks + j])
+        strips_of = turn(loaded[t, j], turns[column * blocks + j])
         for n in range(strips):
             turned[t, n, j] = strips_of[n]
 
-    def turn_first(j, _):
-        turn_block(0, 2 * j)
-        turn_block(0, 2 * j + 1)
-        return 0
-
-    lax.fori_loop(0, blocks // 2, turn_first, 0)
+    for i in range(PIECES):
+        load(0, i).wait()
+        if i == 1:
+            to_scalars.start()
+
+        def turn_first(j, _):
+            turn_block(0, i * third + 2 * j)
+            turn_block(0, i * third + 2 * j + 1)
+            return 0
+
+        lax.fori_loop(0, third // 2, turn_first, 0)
+    for t in range(1, times):
+        for i in range(PIECES):
+            load(t, i).wait()
+    to_scalars.wait()
 
     def pack(m):
         for p in range(columns * MOST):
-            packed[m, p] = turned[m // strips, m % strips, send[p]]
+            packed[m, p] = turned[m // strips, m % strips, table[0, HALF + p]]
 
     def send_column(m):
-        def body(d, _):
-            peer = lax.rem(column + d, columns)
+        for dx, dy in offsets(columns):
+            width = math.isqrt(columns)
+            peer = lax.rem(column // width + dx, width) * width + lax.rem(column % width + dy, width)
             pltpu.make_async_remote_copy(
                 src_ref=packed.at[m, pl.ds(peer * MOST, MOST)],
                 dst_ref=arrived.at[m, pl.ds(column * MOST, MOST)],
@@ -92,9 +166,6 @@
                 recv_sem=xr.at[m],
                 device_id={"gx": peer},
             ).start()
-            return 0
-
-        lax.fori_loop(1, columns, body, 0)
 
     def column_whole(m):
         width = (columns - 1) * MOST
@@ -139,7 +210,7 @@
             staged[column * MOST + q] = packed[m, column * MOST + q]
         for r in range(rows):
             for s in range(capacity):
-                outgoing[m, r, s] = staged[pick[r * capacity + s]]
+                outgoing[m, r, s] = staged[table[0, r * capacity + s]]
         here = landing(row, m)
         for s in range(capacity):
             here[s] = outgoing[m, row, s]
@@ -221,24 +292,6 @@
         put(s).wait()
 
 
-def tables(patch_zone, patch_position, columns, rows, capacity):
-    total = patch_zone.shape[0]
-    blocks = total // columns
-    me = lax.axis_index("gx")
-    block = jnp.arange(total, dtype=jnp.int32)
-    group = block // blocks
-    key = group * columns + patch_zone // rows
-    before = (key[None, :] == key[:, None]) & (block[None, :] < block[:, None])
-    rank = jnp.sum(jnp.where(before, 1, 0), axis=1)
-    place = patch_zone * capacity + patch_position - me * (rows * capacity)
-    target = jnp.arange(rows * capacity, dtype=jnp.int32)
-    pick = jnp.sum(jnp.where(place[None, :] == target[:, None], (group * MOST + rank)[None, :], 0), axis=1)
-    slot = jnp.where(group == me, (patch_zone // rows) * MOST + rank, -1)
-    out_slot = jnp.arange(columns * MOST, dtype=jnp.int32)
-    send = jnp.sum(jnp.where(slot[None, :] == out_slot[:, None], (block - me * blocks)[None, :], 0), axis=1)
-    return send.astype(jnp.int32), pick.astype(jnp.int32)
-
-
 def on_device(field, patch_zone, patch_position, spins, tally):
     times, blocks, side, _ = field.shape
     columns = lax.axis_size("gx")
@@ -246,21 +299,31 @@
     capacity = 2 * blocks // rows
     strips = side // 8
     chunks = times * strips
-    send, pick = tables(patch_zone, patch_position, columns, rows, capacity)
     smem = pl.BlockSpec(memory_space=pltpu.SMEM)
     vmem = pl.BlockSpec(memory_space=pltpu.VMEM)
+    hbm = pl.BlockSpec(memory_space=pltpu.HBM)
+    lines = patch_zone.shape[0] // 128
     anywhere = pl.BlockSpec(memory_space=pl.ANY)
+    operands = (patch_zone.reshape(lines, 128), patch_position.reshape(lines, 128), spins, field)
     arrived = pl.pallas_call(
         functools.partial(exchange_kernel, columns, rows),
         out_shape=pltpu.VMEM((rows, times, capacity, side, side), jnp.float32),
-        in_specs=[smem, smem, smem, vmem],
+        in_specs=[hbm, hbm, hbm, hbm],
         out_specs=vmem,
         scratch_shapes=[
+            pltpu.VMEM((lines, 128), jnp.int32),
+            pltpu.VMEM((lines, 128), jnp.int32),
+            pltpu.VMEM((1, 128), jnp.int32),
+            pltpu.SMEM((1, 128), jnp.int32),
+            pltpu.SMEM(spins.shape, jnp.int32),
+            pltpu.VMEM((times, blocks, side, side), jnp.float32),
             pltpu.VMEM((times, strips, blocks, 8, side), jnp.float32),
             pltpu.VMEM((chunks, columns * MOST, 8, side), jnp.float32),
             pltpu.VMEM((chunks, columns * MOST, 8, side), jnp.float32),
             pltpu.VMEM((columns * MOST, 8, side), jnp.float32),
             pltpu.VMEM((chunks, rows, capacity, 8, side), jnp.float32),
+            pltpu.SemaphoreType.DMA((4,)),
+            pltpu.SemaphoreType.DMA((times, PIECES)),
             pltpu.SemaphoreType.DMA((chunks,)),
             pltpu.SemaphoreType.DMA((chunks,)),
             pltpu.SemaphoreType.DMA((chunks,)),
@@ -270,7 +333,7 @@
             collective_id=0, has_side_effects=True, vmem_limit_bytes=36 * 2**20
         ),
         name="exchange",
-    )(send, pick, spins, pltpu.with_memory_space_constraint(field, pltpu.VMEM))
+    )(*(pltpu.with_memory_space_constraint(a, pltpu.HBM) for a in operands))
     regional = arrived.reshape(rows * times, capacity, side, side)
     centred = pl.pallas_call(
         centre_kernel,

time: 94.4 us -> 89.6 us (0.949)
  local copies, waits for them, and re-layouts: 2.57 us -> 0 us
  other arithmetic: 1.77 us -> 0 us
    unnamed x4 -> x0, local copies, waits for them, and re-layouts: 2.57 us -> none
where the time goes in v3:
time: 89.6 us; the launch traced here: 89.5 us
  Pallas kernels  88.8 us (99%)
    pallas_call x1, Pallas kernels, on_device(): pl.pallas_call(functools.partial(exchange_kernel, columns, rows), out_sha...  85.9 us
    pallas_call x1, Pallas kernels, on_device(): pl.pallas_call(centre_kernel, out_shape=jax.ShapeDtypeStruct((rows * time...  2.94 us

profile of v3, /device:TPU:1, one launch (start us, length us, event | category | flops | bytes accessed | tf_op | source)
XLA Modules:
  0.0 89.5 jit_solution(891514701822888254)
XLA Ops:
  0.7 85.9 %exchange.1 = f32[8,2,6,128,128]{4,3,2,1,0:T(8,128)S(1)} custom-call(s32[3,128]{1,0:T(4,128)} %bitcast.7, s32[3,128]{1,0:T(4,128)} %bitcast.8, s32[384]{0:T(512)} %spins.1, f32[2,24,128,128]{3,2,1,0:T(8,128)} %field.1), custom_call_target="tpu_custom_call" | custom-call | tf_op jit(solution)/shard_map/exchange/pallas_call | solution.py:308
  86.6 2.9 %centre.1 = f32[16,6,128,128]{3,2,1,0:T(8,128)} custom-call(s32[1]{0:T(128)S(6)} %copy.7.tally, f32[16,6,128,128]{3,2,1,0:T(8,128)S(1)} %bitcast.6), custom_call_target="tpu_custom_call" | custom-call | tf_op jit(solution)/shard_map/centre/pallas_call | solution.py:338

commit v4 on v3

--- a/solution.py
+++ b/solution.py
@@ -11,7 +11,9 @@
 MOST = 3
 AHEAD = 6
 HALF = 64
-PIECES = 4
+USED = HALF - 1
+LAG = 4
+PIECES = 3
 TURNS = 3
 
 
@@ -71,13 +73,16 @@
     place = jnp.where((place >= 0) & (place < rows * capacity), place, -1)
     slot = jnp.where(group == me, column * MOST + rank + HALF, -1)
     pad = jnp.full((4 - zone.shape[0], 128), -1, jnp.int32)
+    region = me * rows + lax.axis_index("gy")
     both = jnp.concatenate([place, pad, slot, pad], axis=0).T
+    ours = jnp.concatenate([jnp.where(zone == region, USED, -1), pad, pad, pad, pad, pad], axis=0).T
     values = jnp.concatenate([group * MOST + rank, pad, within, pad], axis=0).T
     lane = lax.broadcasted_iota(jnp.int32, (128, 128), 1)
     total = jnp.zeros((128, 128), jnp.int32)
     for i in range(zone.shape[0]):
         for k in (i, 4 + i):
             total += jnp.where(both[:, k : k + 1] == lane, values[:, k : k + 1], 0)
+        total += jnp.where(ours[:, i : i + 1] == lane, 1, 0)
     found = jnp.sum(total, axis=0, keepdims=True)
     last = jnp.where(lane[:1] < HALF, columns * MOST - 1, blocks - 1)
     return jnp.minimum(found, last)
@@ -140,12 +145,8 @@
         if i == 1:
             to_scalars.start()
 
-        def turn_first(j, _):
-            turn_block(0, i * third + 2 * j)
-            turn_block(0, i * third + 2 * j + 1)
-            return 0
-
-        lax.fori_loop(0, third // 2, turn_first, 0)
+        for j in range(third):
+            turn_block(0, i * third + j)
     for t in range(1, times):
         for i in range(PIECES):
             load(t, i).wait()
@@ -215,6 +216,19 @@
         for s in range(capacity):
             here[s] = outgoing[m, row, s]
 
+    def centre(n):
+        epochs = [(r, t) for r in range(rows) for t in range(times)]
+        at = pl.ds(n * 8, 8)
+        for s in range(capacity):
+            values = [result[r, t, s, at, :] for r, t in epochs]
+            level = values
+            while len(level) > 1:
+                level = [a + b for a, b in zip(level[::2], level[1::2])]
+            mean = level[0] * jnp.float32(1.0 / len(epochs))
+            used = s < table[0, USED]
+            for (r, t), value in zip(epochs, values):
+                result[r, t, s, at, :] = jnp.where(used, value - mean, 0.0)
+
     pl.semaphore_wait(barrier, columns + rows - 2)
 
     def ahead(m, _):
@@ -243,53 +257,42 @@
             send_column(m + AHEAD)
 
         send_row(m)
+
+        @pl.when(m >= LAG)
+        def _():
+            row_whole(m - LAG).wait_recv()
+
+        @pl.when(m >= LAG + chunks - strips)
+        def _():
+            centre(m - LAG - (chunks - strips))
+
         return 0
 
     lax.fori_loop(0, chunks, step, 0)
+
+    def finish(m, _):
+        row_whole(m).wait_recv()
+        centre(m - (chunks - strips))
+        return 0
+
+    lax.fori_loop(chunks - LAG, chunks, finish, 0)
 
     def drain(m, _):
         column_whole(m).wait_send()
-        row_whole(m).wait()
+        row_whole(m).wait_send()
         return 0
 
     lax.fori_loop(0, chunks, drain, 0)
 
 
-def centre_kernel(tally, regional, result, centred, out_sem):
-    epochs, capacity, side, _ = regional.shape
-
-    def put(s):
-        return pltpu.make_async_copy(centred.at[:, s], result.at[:, s], out_sem.at[s])
-
-    for s in range(capacity):
-
-        @pl.when(s < tally[0])
-        def _():
-            def strip(n, _):
-                at = pl.ds(n * 8, 8)
-                values = [regional[e, s, at, :] for e in range(epochs)]
-                level = values
-                while len(level) > 1:
-                    level = [a + b for a, b in zip(level[::2], level[1::2])]
-                mean = level[0] * jnp.float32(1.0 / epochs)
-                for e in range(epochs):
-                    centred[e, s, at, :] = values[e] - mean
-                return 0
-
-            lax.fori_loop(0, side // 8, strip, 0, unroll=2)
-
-        @pl.when(s >= tally[0])
-        def _():
-            def strip(n, _):
-                for e in range(epochs):
-                    centred[e, s, pl.ds(n * 8, 8), :] = jnp.zeros((8, side), jnp.float32)
-                return 0
-
-            lax.fori_loop(0, side // 8, strip, 0, unroll=2)
-
-        put(s).start()
-    for s in range(capacity):
-        put(s).wait()
+def write_kernel(regional, result, sem):
+    copies = [
+        pltpu.make_async_copy(regional.at[e], result.at[e], sem.at[e]) for e in range(regional.shape[0])
+    ]
+    for copy in copies:
+        copy.start()
+    for copy in copies:
+        copy.wait()
 
 
 def on_device(field, patch_zone, patch_position, spins, tally):
@@ -299,7 +302,6 @@
     capacity = 2 * blocks // rows
     strips = side // 8
     chunks = times * strips
-    smem = pl.BlockSpec(memory_space=pltpu.SMEM)
     vmem = pl.BlockSpec(memory_space=pltpu.VMEM)
     hbm = pl.BlockSpec(memory_space=pltpu.HBM)
     lines = patch_zone.shape[0] // 128
@@ -335,19 +337,16 @@
         name="exchange",
     )(*(pltpu.with_memory_space_constraint(a, pltpu.HBM) for a in operands))
     regional = arrived.reshape(rows * times, capacity, side, side)
-    centred = pl.pallas_call(
-        centre_kernel,
-        out_shape=jax.ShapeDtypeStruct((rows * times, capacity, side, side), jnp.float32),
-        in_specs=[smem, vmem],
+    written = pl.pallas_call(
+        write_kernel,
+        out_shape=jax.ShapeDtypeStruct(regional.shape, jnp.float32),
+        in_specs=[vmem],
         out_specs=anywhere,
-        scratch_shapes=[
-            pltpu.VMEM((rows * times, capacity, side, side), jnp.float32),
-            pltpu.SemaphoreType.DMA((capacity,)),
-        ],
-        compiler_params=pltpu.CompilerParams(vmem_limit_bytes=20 * 2**20),
-        name="centre",
-    )(tally, regional)
-    return centred[:, None]
+        scratch_shapes=[pltpu.SemaphoreType.DMA((rows * times,))],
+        compiler_params=pltpu.CompilerParams(vmem_limit_bytes=8 * 2**20),
+        name="write",
+    )(regional)
+    return written[:, None]
 
 
 def solution(mesh):

time: 89.6 us -> 88.2 us (0.984)
  no operation moved by 1% of the time
where the time goes in v4:
time: 88.2 us; the launch traced here: 88.1 us
  Pallas kernels  88.1 us (100%)
    pallas_call x1, Pallas kernels, on_device(): pl.pallas_call(functools.partial(exchange_kernel, columns, rows), out_sha...  85.3 us
    pallas_call x1, Pallas kernels, on_device(): pl.pallas_call(write_kernel, out_shape=jax.ShapeDtypeStruct(regional.shap...  2.78 us

profile of v4, /device:TPU:1, one launch (start us, length us, event | category | flops | bytes accessed | tf_op | source)
XLA Modules:
  0.0 88.1 jit_solution(1761161121919418680)
XLA Ops:
  0.0 85.3 %exchange.1 = f32[8,2,6,128,128]{4,3,2,1,0:T(8,128)S(1)} custom-call(s32[3,128]{1,0:T(4,128)} %bitcast.7, s32[3,128]{1,0:T(4,128)} %bitcast.8, s32[384]{0:T(512)} %spins.1, f32[2,24,128,128]{3,2,1,0:T(8,128)} %field.1), custom_call_target="tpu_custom_call" | custom-call | tf_op jit(solution)/shard_map/exchange/pallas_call | solution.py:310
  85.3 2.8 %write.1 = f32[16,6,128,128]{3,2,1,0:T(8,128)} custom-call(f32[16,6,128,128]{3,2,1,0:T(8,128)S(1)} %bitcast.6), custom_call_target="tpu_custom_call" | custom-call | tf_op jit(solution)/shard_map/write/pallas_call | solution.py:340

commit v5 on v4

--- a/solution.py
+++ b/solution.py
@@ -9,10 +9,9 @@
 from jax.sharding import PartitionSpec as P
 
 MOST = 3
-AHEAD = 6
-HALF = 64
-USED = HALF - 1
-LAG = 4
+AHEAD = 8
+USED = 64
+LAG = 6
 PIECES = 3
 TURNS = 3
 
@@ -60,8 +59,23 @@
     return jnp.where(lane >= d, pltpu.roll(flat, d, 1), pltpu.roll(above, d, 1))
 
 
-def tables(zone, place, columns, rows, blocks, capacity):
+def outgoing_table(zone, columns, rows, blocks):
+    base = lax.axis_index("gx") * blocks
+    lane = lax.broadcasted_iota(jnp.int32, (1, 128), 1)
+    column = lane // MOST
+    left = lane - column * MOST
+    held = jnp.zeros((1, 128), jnp.int32)
+    for j in range(blocks):
+        at = base + j
+        same = column == zone[at // 128, at % 128] // rows
+        held = jnp.where(same & (left == 0), j, held)
+        left = jnp.where(same, left - 1, left)
+    return held
+
+
+def arriving_table(zone, place, columns, rows, blocks, capacity):
     me = lax.axis_index("gx")
+    region = me * rows + lax.axis_index("gy")
     line = lax.broadcasted_iota(jnp.int32, zone.shape, 0) * 128 + lax.broadcasted_iota(jnp.int32, zone.shape, 1)
     group = line // blocks
     within = line - group * blocks
@@ -71,26 +85,21 @@
         rank += jnp.where((within >= d) & (earlier(column, d) == column), 1, 0)
     place = zone * capacity + place - me * (rows * capacity)
     place = jnp.where((place >= 0) & (place < rows * capacity), place, -1)
-    slot = jnp.where(group == me, column * MOST + rank + HALF, -1)
+    ours = jnp.where(zone == region, USED, -1)
     pad = jnp.full((4 - zone.shape[0], 128), -1, jnp.int32)
-    region = me * rows + lax.axis_index("gy")
-    both = jnp.concatenate([place, pad, slot, pad], axis=0).T
-    ours = jnp.concatenate([jnp.where(zone == region, USED, -1), pad, pad, pad, pad, pad], axis=0).T
-    values = jnp.concatenate([group * MOST + rank, pad, within, pad], axis=0).T
+    both = jnp.concatenate([place, pad, ours, pad], axis=0).T
+    values = jnp.concatenate([group * MOST + rank, pad, pad, pad, pad, pad], axis=0).T
     lane = lax.broadcasted_iota(jnp.int32, (128, 128), 1)
     total = jnp.zeros((128, 128), jnp.int32)
     for i in range(zone.shape[0]):
-        for k in (i, 4 + i):
-            total += jnp.where(both[:, k : k + 1] == lane, values[:, k : k + 1], 0)
-        total += jnp.where(ours[:, i : i + 1] == lane, 1, 0)
-    found = jnp.sum(total, axis=0, keepdims=True)
-    last = jnp.where(lane[:1] < HALF, columns * MOST - 1, blocks - 1)
-    return jnp.minimum(found, last)
+        total += jnp.where(both[:, i : i + 1] == lane, values[:, i : i + 1], 0)
+        total += jnp.where(both[:, 4 + i : 5 + i] == lane, 1, 0)
+    return jnp.minimum(jnp.sum(total, axis=0, keepdims=True), columns * MOST - 1)
 
 
 def exchange_kernel(
     columns, rows, zone, place, spins, field, result,
-    zone_v, place_v, table_v, table, turns, loaded, turned, packed, arrived, staged, outgoing,
+    zone_v, place_v, zone_s, table_v, send, pick, turns, loaded, turned, packed, arrived, staged, outgoing,
     small_sem, load_sem, xs, xr, zs, zr,
 ):
     times, blocks, side, _ = loaded.shape
@@ -102,9 +111,10 @@
     third = blocks // PIECES
 
     small = [
-        pltpu.make_async_copy(zone, zone_v, small_sem.at[0]),
-        pltpu.make_async_copy(place, place_v, small_sem.at[1]),
-        pltpu.make_async_copy(spins, turns, small_sem.at[2]),
+        pltpu.make_async_copy(zone, zone_s, small_sem.at[0]),
+        pltpu.make_async_copy(spins, turns, small_sem.at[1]),
+        pltpu.make_async_copy(zone, zone_v, small_sem.at[2]),
+        pltpu.make_async_copy(place, place_v, small_sem.at[3]),
     ]
     for copy in small:
         copy.start()
@@ -130,10 +140,11 @@
     lax.fori_loop(1, columns, greet_column, 0)
     lax.fori_loop(1, rows, greet_row, 0)
 
-    for copy in small:
+    for copy in small[:2]:
         copy.wait()
-    table_v[...] = tables(zone_v[...], place_v[...], columns, rows, blocks, capacity)
-    to_scalars = pltpu.make_async_copy(table_v, table, small_sem.at[3])
+    table_v[0] = outgoing_table(zone_s, columns, rows, blocks)
+    to_send = pltpu.make_async_copy(table_v.at[0], send, small_sem.at[4])
+    to_pick = pltpu.make_async_copy(table_v.at[1], pick, small_sem.at[5])
 
     def turn_block(t, j):
         strips_of = turn(loaded[t, j], turns[column * blocks + j])
@@ -143,18 +154,15 @@
     for i in range(PIECES):
         load(0, i).wait()
         if i == 1:
-            to_scalars.start()
+            to_send.start()
 
         for j in range(third):
             turn_block(0, i * third + j)
-    for t in range(1, times):
-        for i in range(PIECES):
-            load(t, i).wait()
-    to_scalars.wait()
+    to_send.wait()
 
     def pack(m):
         for p in range(columns * MOST):
-            packed[m, p] = turned[m // strips, m % strips, table[0, HALF + p]]
+            packed[m, p] = turned[m // strips, m % strips, send[0, p]]
 
     def send_column(m):
         for dx, dy in offsets(columns):
@@ -182,7 +190,7 @@
         return result.at[r, m // strips, :, pl.ds((m % strips) * 8, 8), :]
 
     def send_row(m):
-        def body(d, _):
+        for d in sorted(range(1, rows), key=lambda d: -min(d, rows - d)):
             peer = lax.rem(row + d, rows)
             pltpu.make_async_remote_copy(
                 src_ref=outgoing.at[m, peer],
@@ -191,9 +199,6 @@
                 recv_sem=zr.at[m],
                 device_id={"gy": peer},
             ).start()
-            return 0
-
-        lax.fori_loop(1, rows, body, 0)
 
     def row_whole(m):
         return pltpu.make_async_remote_copy(
@@ -211,7 +216,7 @@
             staged[column * MOST + q] = packed[m, column * MOST + q]
         for r in range(rows):
             for s in range(capacity):
-                outgoing[m, r, s] = staged[table[0, r * capacity + s]]
+                outgoing[m, r, s] = staged[pick[0, r * capacity + s]]
         here = landing(row, m)
         for s in range(capacity):
             here[s] = outgoing[m, row, s]
@@ -225,7 +230,7 @@
             while len(level) > 1:
                 level = [a + b for a, b in zip(level[::2], level[1::2])]
             mean = level[0] * jnp.float32(1.0 / len(epochs))
-            used = s < table[0, USED]
+            used = s < pick[0, USED]
             for (r, t), value in zip(epochs, values):
                 result[r, t, s, at, :] = jnp.where(used, value - mean, 0.0)
 
@@ -237,26 +242,35 @@
         return 0
 
     lax.fori_loop(0, AHEAD, ahead, 0)
+    pack(AHEAD)
+    for copy in small[2:]:
+        copy.wait()
+    table_v[1] = arriving_table(zone_v[...], place_v[...], columns, rows, blocks, capacity)
+    for t in range(1, times):
+        for i in range(PIECES):
+            load(t, i).wait()
+    to_pick.start()
+    to_pick.wait()
 
     def step(m, _):
+        column_whole(m).wait_recv()
+        select(m)
+
+        @pl.when(m + AHEAD < chunks)
+        def _():
+            send_column(m + AHEAD)
+
+        send_row(m)
+
         @pl.when(m < (times - 1) * blocks // TURNS)
         def _():
             for i in range(TURNS):
                 at = m * TURNS + i
                 turn_block(1 + at // blocks, at % blocks)
 
-        @pl.when(m + AHEAD < chunks)
-        def _():
-            pack(m + AHEAD)
-
-        column_whole(m).wait_recv()
-        select(m)
-
-        @pl.when(m + AHEAD < chunks)
-        def _():
-            send_column(m + AHEAD)
-
-        send_row(m)
+        @pl.when(m + AHEAD + 1 < chunks)
+        def _():
+            pack(m + AHEAD + 1)
 
         @pl.when(m >= LAG)
         def _():
@@ -286,13 +300,9 @@
 
 
 def write_kernel(regional, result, sem):
-    copies = [
-        pltpu.make_async_copy(regional.at[e], result.at[e], sem.at[e]) for e in range(regional.shape[0])
-    ]
-    for copy in copies:
-        copy.start()
-    for copy in copies:
-        copy.wait()
+    copy = pltpu.make_async_copy(regional, result, sem)
+    copy.start()
+    copy.wait()
 
 
 def on_device(field, patch_zone, patch_position, spins, tally):
@@ -315,7 +325,9 @@
         scratch_shapes=[
             pltpu.VMEM((lines, 128), jnp.int32),
             pltpu.VMEM((lines, 128), jnp.int32),
-            pltpu.VMEM((1, 128), jnp.int32),
+            pltpu.SMEM((lines, 128), jnp.int32),
+            pltpu.VMEM((2, 1, 128), jnp.int32),
+            pltpu.SMEM((1, 128), jnp.int32),
             pltpu.SMEM((1, 128), jnp.int32),
             pltpu.SMEM(spins.shape, jnp.int32),
             pltpu.VMEM((times, blocks, side, side), jnp.float32),
@@ -324,7 +336,7 @@
             pltpu.VMEM((chunks, columns * MOST, 8, side), jnp.float32),
             pltpu.VMEM((columns * MOST, 8, side), jnp.float32),
             pltpu.VMEM((chunks, rows, capacity, 8, side), jnp.float32),
-            pltpu.SemaphoreType.DMA((4,)),
+            pltpu.SemaphoreType.DMA((6,)),
             pltpu.SemaphoreType.DMA((times, PIECES)),
             pltpu.SemaphoreType.DMA((chunks,)),
             pltpu.SemaphoreType.DMA((chunks,)),
@@ -342,7 +354,7 @@
         out_shape=jax.ShapeDtypeStruct(regional.shape, jnp.float32),
         in_specs=[vmem],
         out_specs=anywhere,
-        scratch_shapes=[pltpu.SemaphoreType.DMA((rows * times,))],
+        scratch_shapes=[pltpu.SemaphoreType.DMA],
         compiler_params=pltpu.CompilerParams(vmem_limit_bytes=8 * 2**20),
         name="write",
     )(regional)

time: 88.2 us -> 87 us (0.986)
  Pallas kernels: 88.1 us -> 86.9 us
    pallas_call x1, Pallas kernels: 85.3 us -> 84.2 us  [on_device(): pl.pallas_call(functools.partial(exchange_kernel, columns, rows), out_sha...]
where the time goes in v5:
time: 87 us; the launch traced here: 86.9 us
  Pallas kernels  86.9 us (100%)
    pallas_call x1, Pallas kernels, on_device(): pl.pallas_call(functools.partial(exchange_kernel, columns, rows), out_sha...  84.2 us
    pallas_call x1, Pallas kernels, on_device(): pl.pallas_call(write_kernel, out_shape=jax.ShapeDtypeStruct(regional.shap...  2.71 us

profile of v5, /device:TPU:1, one launch (start us, length us, event | category | flops | bytes accessed | tf_op | source)
XLA Modules:
  0.0 86.9 jit_solution(13747558598439697614)
XLA Ops:
  0.0 84.2 %exchange.1 = f32[8,2,6,128,128]{4,3,2,1,0:T(8,128)S(1)} custom-call(s32[3,128]{1,0:T(4,128)} %bitcast.7, s32[3,128]{1,0:T(4,128)} %bitcast.8, s32[384]{0:T(512)} %spins.1, f32[2,24,128,128]{3,2,1,0:T(8,128)} %field.1), custom_call_target="tpu_custom_call" | custom-call | tf_op jit(solution)/shard_map/exchange/pallas_call | solution.py:320
  84.2 2.7 %write.1 = f32[16,6,128,128]{3,2,1,0:T(8,128)} custom-call(f32[16,6,128,128]{3,2,1,0:T(8,128)S(1)} %bitcast.6), custom_call_target="tpu_custom_call" | custom-call | tf_op jit(solution)/shard_map/write/pallas_call | solution.py:352

commit v6 on v5

--- a/solution.py
+++ b/solution.py
@@ -9,11 +9,11 @@
 from jax.sharding import PartitionSpec as P
 
 MOST = 3
-AHEAD = 8
+AHEAD = 4
 USED = 64
 LAG = 6
 PIECES = 3
-TURNS = 3
+TURNS = 2
 
 
 def offsets(columns):
@@ -164,10 +164,13 @@
         for p in range(columns * MOST):
             packed[m, p] = turned[m // strips, m % strips, send[0, p]]
 
+    core = lax.rem(row, 2)
+
     def send_column(m):
         for dx, dy in offsets(columns):
             width = math.isqrt(columns)
-            peer = lax.rem(column // width + dx, width) * width + lax.rem(column % width + dy, width)
+            across, down = core * dx + (1 - core) * dy, core * dy + (1 - core) * dx
+            peer = lax.rem(column // width + across, width) * width + lax.rem(column % width + down, width)
             pltpu.make_async_remote_copy(
                 src_ref=packed.at[m, pl.ds(peer * MOST, MOST)],
                 dst_ref=arrived.at[m, pl.ds(column * MOST, MOST)],
@@ -284,19 +287,21 @@
 
     lax.fori_loop(0, chunks, step, 0)
 
-    def finish(m, _):
-        row_whole(m).wait_recv()
-        centre(m - (chunks - strips))
-        return 0
-
-    lax.fori_loop(chunks - LAG, chunks, finish, 0)
-
     def drain(m, _):
         column_whole(m).wait_send()
         row_whole(m).wait_send()
         return 0
 
-    lax.fori_loop(0, chunks, drain, 0)
+    lax.fori_loop(0, chunks - LAG, drain, 0)
+
+    def finish(m, _):
+        column_whole(m).wait_send()
+        row_whole(m).wait_send()
+        row_whole(m).wait_recv()
+        centre(m - (chunks - strips))
+        return 0
+
+    lax.fori_loop(chunks - LAG, chunks, finish, 0)
 
 
 def write_kernel(regional, result, sem):

time: 87 us -> 86.7 us (level)
  no operation moved by 1% of the time
where the time goes in v6:
time: 86.7 us; the launch traced here: 86.6 us
  Pallas kernels  86.6 us (100%)
    pallas_call x1, Pallas kernels, on_device(): pl.pallas_call(functools.partial(exchange_kernel, columns, rows), out_sha...  83.9 us
    pallas_call x1, Pallas kernels, on_device(): pl.pallas_call(write_kernel, out_shape=jax.ShapeDtypeStruct(regional.shap...  2.71 us

profile of v6, /device:TPU:1, one launch (start us, length us, event | category | flops | bytes accessed | tf_op | source)
XLA Modules:
  0.0 86.6 jit_solution(3854260790803335768)
XLA Ops:
  0.0 83.9 %exchange.1 = f32[8,2,6,128,128]{4,3,2,1,0:T(8,128)S(1)} custom-call(s32[3,128]{1,0:T(4,128)} %bitcast.7, s32[3,128]{1,0:T(4,128)} %bitcast.8, s32[384]{0:T(512)} %spins.1, f32[2,24,128,128]{3,2,1,0:T(8,128)} %field.1), custom_call_target="tpu_custom_call" | custom-call | tf_op jit(solution)/shard_map/exchange/pallas_call | solution.py:325
  83.9 2.7 %write.1 = f32[16,6,128,128]{3,2,1,0:T(8,128)} custom-call(f32[16,6,128,128]{3,2,1,0:T(8,128)S(1)} %bitcast.6), custom_call_target="tpu_custom_call" | custom-call | tf_op jit(solution)/shard_map/write/pallas_call | solution.py:357

commit v7 on v6

--- a/solution.py
+++ b/solution.py
@@ -12,7 +12,7 @@
 AHEAD = 4
 USED = 64
 LAG = 6
-PIECES = 3
+PIECES = 2
 TURNS = 2
 
 
@@ -108,7 +108,7 @@
     capacity = outgoing.shape[2]
     column = lax.axis_index("gx")
     row = lax.axis_index("gy")
-    third = blocks // PIECES
+    part = blocks // PIECES
 
     small = [
         pltpu.make_async_copy(zone, zone_s, small_sem.at[0]),
@@ -120,7 +120,7 @@
         copy.start()
 
     def load(t, i):
-        cut = pl.ds(i * third, third)
+        cut = pl.ds(i * part, part)
         return pltpu.make_async_copy(field.at[t, cut], loaded.at[t, cut], load_sem.at[t, i])
 
     for t in range(times):
@@ -151,13 +151,18 @@
         for n in range(strips):
             turned[t, n, j] = strips_of[n]
 
-    for i in range(PIECES):
+    def turn_piece(i, _):
         load(0, i).wait()
-        if i == 1:
+
+        @pl.when(i == 1)
+        def _():
             to_send.start()
 
-        for j in range(third):
-            turn_block(0, i * third + j)
+        for j in range(part):
+            turn_block(0, i * part + j)
+        return 0
+
+    lax.fori_loop(0, PIECES, turn_piece, 0)
     to_send.wait()
 
     def pack(m):
@@ -192,16 +197,14 @@
     def landing(r, m):
         return result.at[r, m // strips, :, pl.ds((m % strips) * 8, 8), :]
 
-    def send_row(m):
-        for d in sorted(range(1, rows), key=lambda d: -min(d, rows - d)):
-            peer = lax.rem(row + d, rows)
-            pltpu.make_async_remote_copy(
-                src_ref=outgoing.at[m, peer],
-                dst_ref=landing(row, m),
-                send_sem=zs.at[m],
-                recv_sem=zr.at[m],
-                device_id={"gy": peer},
-            ).start()
+    def send_row(m, peer):
+        pltpu.make_async_remote_copy(
+            src_ref=outgoing.at[m, peer],
+            dst_ref=landing(row, m),
+            send_sem=zs.at[m],
+            recv_sem=zr.at[m],
+            device_id={"gy": peer},
+        ).start()
 
     def row_whole(m):
         return pltpu.make_async_remote_copy(
@@ -217,12 +220,18 @@
             staged[a] = arrived[m, a]
         for q in range(MOST):
             staged[column * MOST + q] = packed[m, column * MOST + q]
-        for r in range(rows):
+        waiting = None
+        for d in sorted(range(1, rows), key=lambda d: -min(d, rows - d)):
+            peer = lax.rem(row + d, rows)
             for s in range(capacity):
-                outgoing[m, r, s] = staged[pick[0, r * capacity + s]]
+                outgoing[m, peer, s] = staged[pick[0, peer * capacity + s]]
+            if waiting is not None:
+                send_row(m, waiting)
+            waiting = peer
         here = landing(row, m)
         for s in range(capacity):
-            here[s] = outgoing[m, row, s]
+            here[s] = staged[pick[0, row * capacity + s]]
+        send_row(m, waiting)
 
     def centre(n):
         epochs = [(r, t) for r in range(rows) for t in range(times)]
@@ -262,8 +271,6 @@
         @pl.when(m + AHEAD < chunks)
         def _():
             send_column(m + AHEAD)
-
-        send_row(m)
 
         @pl.when(m < (times - 1) * blocks // TURNS)
         def _():

time: 86.7 us -> 86.9 us (level)
  no operation moved by 1% of the time
where the time goes in v7:
time: 86.9 us; the launch traced here: 86.8 us
  Pallas kernels  86.8 us (100%)
    pallas_call x1, Pallas kernels, on_device(): pl.pallas_call(functools.partial(exchange_kernel, columns, rows), out_sha...  84.1 us
    pallas_call x1, Pallas kernels, on_device(): pl.pallas_call(write_kernel, out_shape=jax.ShapeDtypeStruct(regional.shap...  2.71 us

profile of v7, /device:TPU:1, one launch (start us, length us, event | category | flops | bytes accessed | tf_op | source)
XLA Modules:
  0.0 86.8 jit_solution(18318627125630989917)
XLA Ops:
  0.0 84.1 %exchange.1 = f32[8,2,6,128,128]{4,3,2,1,0:T(8,128)S(1)} custom-call(s32[3,128]{1,0:T(4,128)} %bitcast.7, s32[3,128]{1,0:T(4,128)} %bitcast.8, s32[384]{0:T(512)} %spins.1, f32[2,24,128,128]{3,2,1,0:T(8,128)} %field.1), custom_call_target="tpu_custom_call" | custom-call | tf_op jit(solution)/shard_map/exchange/pallas_call | solution.py:332
  84.1 2.7 %write.1 = f32[16,6,128,128]{3,2,1,0:T(8,128)} custom-call(f32[16,6,128,128]{3,2,1,0:T(8,128)S(1)} %bitcast.6), custom_call_target="tpu_custom_call" | custom-call | tf_op jit(solution)/shard_map/write/pallas_call | solution.py:364
